TPU v7x, 128 devices: a whole 4x4x4 slice. The times are simulated.
128 devices in a mesh: tm: 32 (over y_hi, x, z), lev: 4 (over y_lo, core).
Axes of the slice: x: 4, y: 4 (y_hi: 2, y_lo: 2; y = y_hi * 2 + y_lo), z: 4, core: 2. Of those that a mesh axis runs over, the one named last changes fastest.
Arguments:
- increment: float32 [32, 3, 8, 256, 512], P('tm', None, 'lev'), may hold values from -6 to 6
- multiplier: float32 [32, 3, 8, 256, 512], P('tm', None, 'lev'), may hold values from -6 to 6
- error_var: float32 [32, 3, 8, 256, 512], P('tm', None, 'lev'), may hold values from 0.1 to 1
- obs_cell: int32 [32, 8, 512], P('tm', 'lev'), may hold values from 0 to 131071
- obs_dual: float32 [32, 8, 512], P('tm', 'lev'), may hold values from -6 to 6
- obs_var: float32 [32, 8, 512], P('tm', 'lev'), may hold values from 0.5 to 2
- level_gain: float32 [8], P('lev'), may hold values from 0.5 to 1.5
- mean_depth: float32 [8], P('lev'), may hold values from 0.5 to 2
- chain_decay: float32 [32, 3, 8], P('tm', None, 'lev'), may hold values from 0 to 1
Outputs:
- dual_product: float32 [32, 3, 8, 256, 512], P('tm', None, 'lev')
- obs_product: float32 [32, 8, 512], P('tm', 'lev')
- state_block_product: float32 [32, 3, 8, 256, 512], P('tm', None, 'lev')
- chain_solution: float32 [32, 3, 8, 256, 512], P('tm', None, 'lev')
All inputs are finite; a program needn't handle non-finite values.
Results may differ from a plain program's by a relative error of at most 0.0001.
Values sent between devices are 32-bit elements; how exact they have to be, the bound alone decides.
No kernel may reach another device: no remote copies, remote signals or barrier semaphores. Data moves between devices by JAX's collectives and lax.ppermute only.
A program may use at most 320 MiB of HBM per device.

v0:
```python
import jax
import jax.numpy as jnp
from jax import lax
from jax.experimental import pallas as pl
from jax.experimental.pallas import tpu as pltpu
from jax.sharding import PartitionSpec as P


DT = 0.25
ROT = 0.5
COUP = 0.25
LINE = 4
GX, GY = 256, 512
HALF = GX // 2
SENT = HALF + 8
R = 128
CHUNKS = GX // R
F32 = jnp.float32


def shape(*dims):
    return jax.ShapeDtypeStruct(dims, F32)


def over_rows(body):
    def step(t, carry):
        body(t, pl.multiple_of(t * R, R))
        return carry

    lax.fori_loop(0, CHUNKS, step, 0, unroll=True)


def lanes():
    return lax.broadcasted_iota(jnp.int32, (R, GY), 1)


def next_lane(a):
    return jnp.where(lanes() < GY - 1, pltpu.roll(a, GY - 1, 1), 0.0)


def prev_lane(a):
    return jnp.where(lanes() > 0, pltpu.roll(a, 1, 1), 0.0)


def rows_and_next(ref, r):
    big = ref[pl.ds(r, R + 8), :]
    return big[:R], pltpu.roll(big, R + 7, 0)[:R]


def rows_and_prev(ref, r):
    big = ref[pl.ds(r, R + 8), :]
    return big[8:], pltpu.roll(big, 1, 0)[8:]


def clear_pads(nxt, prv):
    for ref in nxt:
        ref[GX : GX + 8, :] = jnp.zeros((8, GY), F32)
    for ref in prv:
        ref[0:8, :] = jnp.zeros((8, GY), F32)


def forward_step(h, u, v, column, gain, depth, p, un, vn, put):
    def first(t, r):
        here = gain * h(r)
        p[pl.ds(r, R), :] = here if column is None else here + COUP * column(r)

    over_rows(first)

    def second(t, r):
        here, after = rows_and_next(p, r)
        u0, v0 = u(r), v(r)
        un[pl.ds(r + 8, R), :] = u0 + DT * (ROT * v0 - (after - here))
        vn[pl.ds(r, R), :] = v0 - DT * (ROT * u0 + (next_lane(here) - here))

    over_rows(second)

    def third(t, r):
        u1, before = rows_and_prev(un, r)
        v1 = vn[pl.ds(r, R), :]
        put(t, r, h(r) - DT * depth * ((u1 - before) + (v1 - prev_lane(v1))), u1, v1)

    over_rows(third)


def adjoint_step(h, u, v, depth, p, un, vn, put):
    def first(t, r):
        p[pl.ds(r, R), :] = h(r)

    over_rows(first)

    def second(t, r):
        here, after = rows_and_next(p, r)
        un[pl.ds(r + 8, R), :] = u(r) + DT * depth * (after - here)
        vn[pl.ds(r, R), :] = v(r) + DT * depth * (next_lane(here) - here)

    over_rows(second)

    def third(t, r):
        u1, before = rows_and_prev(un, r)
        v1 = vn[pl.ds(r, R), :]
        put(t, r, DT * ((u1 - before) + (v1 - prev_lane(v1))), u1 - DT * ROT * v1, v1 + DT * ROT * u1)

    over_rows(third)


def laplacian_onto(column, extra, total_depth, target):
    def body(t, r):
        here, after = rows_and_next(column, r)
        dx = after - here
        start = jnp.maximum(r - 8, 0)
        edge = column[pl.ds(pl.multiple_of(start, 8), 8), :][7:8]
        rows = lax.broadcasted_iota(jnp.int32, (R, GY), 0)
        before = jnp.where(rows == 0, edge, pltpu.roll(here, 1, 0))
        back = jnp.where(rows + r > 0, here - before, 0.0)
        dy = next_lane(here) - here
        target[pl.ds(r, R), :] = extra(r) + (DT * DT * COUP * total_depth) * ((dx - back) + (dy - prev_lane(dy)))

    over_rows(body)


SCRATCH = [pltpu.VMEM((GX + 8, GY), F32), pltpu.VMEM((GX + 8, GY), F32), pltpu.VMEM((GX, GY), F32)]
STATE = pl.BlockSpec((3, 1, GX, GY), lambda k: (0, k, 0, 0))
QUARTER = GX // 4
SMEM = pl.BlockSpec(memory_space=pltpu.SMEM)


def whole(*dims):
    return pl.BlockSpec(dims, lambda k: (0,) * len(dims))


def cost(micros, moved):
    return pl.CostEstimate(flops=int(micros * 4_000_000), bytes_accessed=moved, transcendentals=0)


def params():
    return pltpu.CompilerParams(dimension_semantics=("arbitrary",), vmem_limit_bytes=67_043_328)


def add_to_half(k, t, core, mine, theirs, slot, value):
    r = pl.multiple_of((t % (CHUNKS // 2)) * R, R)

    def onto(ref):
        @pl.when(k == 0)
        def _():
            ref[slot, pl.ds(r, R), :] = value

        @pl.when(k > 0)
        def _():
            ref[slot, pl.ds(r, R), :] += value

    pl.when(t // (CHUNKS // 2) == core)(lambda: onto(mine))
    pl.when(t // (CHUNKS // 2) != core)(lambda: onto(theirs))


def put_depths(k, depth, *outs):
    @pl.when(k == 0)
    def _():
        for out in outs:
            for slot in range(2):
                out[slot, HALF:SENT, :] = jnp.full((8, GY), depth[0] + depth[1], F32)


def forward_partials_body(core, gain, depth, x, mine, theirs, p, un, vn):
    k = pl.program_id(0)
    put_depths(k, depth, mine, theirs)
    clear_pads([p], [un])

    def put(t, r, h1, u1, v1):
        add_to_half(k, t, core[0], mine, theirs, 0, x[0, 0, pl.ds(r, R), :])
        add_to_half(k, t, core[0], mine, theirs, 1, h1)

    field = lambda f: lambda r: x[f, 0, pl.ds(r, R), :]
    forward_step(field(0), field(1), field(2), None, gain[k], depth[k], p, un, vn, put)


def adjoint_partials_body(core, gain, depth, x, mine, theirs, p, un, vn, h1, u1, v1):
    k = pl.program_id(0)
    put_depths(k, depth, mine, theirs)
    clear_pads([p], [un])
    field = lambda f: lambda r: x[f, 0, pl.ds(r, R), :]
    from_ref = lambda ref: lambda r: ref[pl.ds(r, R), :]

    def put(t, r, ap, a, b):
        add_to_half(k, t, core[0], mine, theirs, 0, ap)
        h1[pl.ds(r, R), :] = x[0, 0, pl.ds(r, R), :] + gain[k] * ap
        u1[pl.ds(r, R), :] = a
        v1[pl.ds(r, R), :] = b

    adjoint_step(field(0), field(1), field(2), depth[k], p, un, vn, put)

    def put_second(t, r, ap, a, b):
        add_to_half(k, t, core[0], mine, theirs, 1, ap)

    adjoint_step(from_ref(h1), from_ref(u1), from_ref(v1), depth[k], p, un, vn, put_second)


def partials(body, core, gain, depth, state, scratch):
    halves = shape(2, SENT, GY)
    return pl.pallas_call(
        body,
        grid=(2,),
        in_specs=[SMEM, SMEM, SMEM, STATE],
        out_specs=[whole(2, SENT, GY)] * 2,
        out_shape=[halves, halves],
        scratch_shapes=scratch,
        compiler_params=params(),
        cost_estimate=cost(4, 4 << 20),
    )(core, gain, depth, state)


def join_columns(core, mine, other, total_depth, column, second):
    def first(t, r):
        s = pl.multiple_of((t % (CHUNKS // 2)) * R, R)

        @pl.when(t // (CHUNKS // 2) == core)
        def _():
            column[pl.ds(r, R), :] = mine[0, pl.ds(s, R), :]
            second[pl.ds(r, R), :] = mine[1, pl.ds(s, R), :]

        @pl.when(t // (CHUNKS // 2) != core)
        def _():
            column[pl.ds(r, R), :] = other[0, pl.ds(s, R), :]
            second[pl.ds(r, R), :] = other[1, pl.ds(s, R), :]

    clear_pads([column], [])
    over_rows(first)
    laplacian_onto(column, lambda r: second[pl.ds(r, R), :], total_depth, second)


def both_forward(x, column, second, gain, depth, p, un, vn, h1, u1, v1, put):
    field = x if callable(x) else lambda f: lambda r: x[f, 0, pl.ds(r, R), :]
    from_ref = lambda ref: lambda r: ref[pl.ds(r, R), :]

    def keep(t, r, h, u, v):
        h1[pl.ds(r, R), :] = h
        u1[pl.ds(r, R), :] = u
        v1[pl.ds(r, R), :] = v

    forward_step(field(0), field(1), field(2), from_ref(column), gain, depth, p, un, vn, keep)
    forward_step(from_ref(h1), from_ref(u1), from_ref(v1), from_ref(second), gain, depth, p, un, vn, put)


def both_adjoint(x, column, second, gain, depth, p, un, vn, h1, u1, v1, put):
    field = x if callable(x) else lambda f: lambda r: x[f, 0, pl.ds(r, R), :]
    from_ref = lambda ref: lambda r: ref[pl.ds(r, R), :]

    def keep(t, r, ap, u, v):
        h1[pl.ds(r, R), :] = field(0)(r) + gain * ap + COUP * column[pl.ds(r, R), :]
        u1[pl.ds(r, R), :] = u
        v1[pl.ds(r, R), :] = v

    def last(t, r, ap, u, v):
        put(t, r, h1[pl.ds(r, R), :] + gain * ap + COUP * second[pl.ds(r, R), :], u, v)

    adjoint_step(field(0), field(1), field(2), depth, p, un, vn, keep)
    adjoint_step(from_ref(h1), from_ref(u1), from_ref(v1), depth, p, un, vn, last)


COLUMN_SCRATCH = [pltpu.VMEM((GX + 8, GY), F32), pltpu.VMEM((GX, GY), F32)]
LEVEL_SCRATCH = [pltpu.VMEM((GX, GY), F32)] * 3
ANY = pl.BlockSpec(memory_space=pl.ANY)


def chain_terms_body(
    core, place, gain, depth, factor, x, lam, ev, mine, other, own_rows, *rest
):
    outs, (p, un, vn, h1, u1, v1, column, second, term) = rest[:LINE], rest[LINE:]
    k = pl.program_id(0)

    @pl.when(k == 0)
    def _():
        clear_pads([p], [un])
        join_columns(core[0], mine, other, mine[0, HALF : HALF + 1, :], column, second)

    def put(t, r, h, u, v):
        for f, moved in enumerate((h, u, v)):
            own = ev[f, 0, pl.ds(r, R), :] * lam[f, 0, pl.ds(r, R), :] + x[f, 0, pl.ds(r, R), :]
            own_rows[f, 0, pl.ds(r, R), :] = own
            term[f, pl.ds(r, R), :] = factor[2 * f + k] * own - moved

    both_forward(x, column, second, gain[k], depth[k], p, un, vn, h1, u1, v1, put)
    for slot, out in enumerate(outs):
        r = pl.multiple_of(lax.rem(place[0] + slot, LINE) * QUARTER, QUARTER)
        for f in range(3):
            out[0, f] = term[f, pl.ds(r, QUARTER), :]


def by_level(*dims):
    return pl.BlockSpec((1,) + dims, lambda k: (k,) + (0,) * len(dims))


PIECES = [by_level(3, QUARTER, GY)] * LINE
PIECE_SHAPES = [shape(2, 3, QUARTER, GY)] * LINE


def chain_terms(core, place, gain, depth, factor, x, lam, ev, mine, other):
    return pl.pallas_call(
        chain_terms_body,
        grid=(2,),
        in_specs=[SMEM] * 5 + [STATE] * 3 + [whole(2, SENT, GY)] * 2,
        out_specs=[STATE] + PIECES,
        out_shape=[shape(3, 2, GX, GY)] + PIECE_SHAPES,
        scratch_shapes=SCRATCH + LEVEL_SCRATCH + COLUMN_SCRATCH + [pltpu.VMEM((3, GX, GY), F32)],
        compiler_params=params(),
        cost_estimate=cost(7, 16 << 20),
        name="chain_terms",
    )(core, place, gain, depth, factor, x, lam, ev, mine, other)


def columns_of(model):
    return pl.BlockSpec((2, HALF, GY), lambda k: (model, 0, 0))


def products_body(
    core, second_way, gain, depth, depths, own, lam, xr, xr2, xv, xv2, lr, lr2, lv, lv2, fm, fo, am, ao, added,
    dual, block, p, un, vn, h1, u1, v1, fc, fs, ac, as_,
):
    k = pl.program_id(0)

    @pl.when(k == 0)
    def _():
        clear_pads([p], [un])
        join_columns(core[0], fm, fo, depths[0, 0:1, :], fc, fs)
        join_columns(core[0], am, ao, depths[0, 0:1, :], ac, as_)

    def arrived(first, second, last, second_last, flag):
        def field(f):
            a, b, i, at = (first, second, f, flag) if f < SENT_FIRST else (last, second_last, f - SENT_FIRST, flag + 1)
            return lambda r: jnp.where(second_way[at] > 0, b[i, 0, pl.ds(r, R), :], a[i, 0, pl.ds(r, R), :])

        return field

    def put(t, r, h, u, v):
        for f, moved in enumerate((h, u, v)):
            dual[f, 0, pl.ds(r, R), :] = own[f, 0, pl.ds(r, R), :] - moved

    both_forward(arrived(xr, xr2, xv, xv2, 0), fc, fs, gain[k], depth[k], p, un, vn, h1, u1, v1, put)

    def put_adjoint(t, r, h, u, v):
        block[0, 0, pl.ds(r, R), :] = (lam[0, 0, pl.ds(r, R), :] - h) + added[0, pl.ds(r, R), :]
        block[1, 0, pl.ds(r, R), :] = lam[1, 0, pl.ds(r, R), :] - u
        block[2, 0, pl.ds(r, R), :] = lam[2, 0, pl.ds(r, R), :] - v

    both_adjoint(arrived(lr, lr2, lv, lv2, 2), ac, as_, gain[k], depth[k], p, un, vn, h1, u1, v1, put_adjoint)


SENT_FIRST = 2


def fields(count):
    return pl.BlockSpec((count, 1, GX, GY), lambda k: (0, k, 0, 0))


def products(core, second_way, gain, depth, depths, own, lam, arrivals, fm, fo, am, ao, added):
    state = shape(3, 2, GX, GY)
    return pl.pallas_call(
        products_body,
        grid=(2,),
        in_specs=[SMEM] * 4
        + [pl.BlockSpec((1, 8, GY), lambda k: (0, HALF // 8, 0))]
        + [STATE] * 2
        + [fields(SENT_FIRST), fields(SENT_FIRST), fields(3 - SENT_FIRST), fields(3 - SENT_FIRST)] * 2
        + [columns_of(0), columns_of(0), columns_of(1), columns_of(1)]
        + [pl.BlockSpec((1, GX, GY), lambda k: (k, 0, 0))],
        out_specs=[STATE] * 2,
        out_shape=[state, state],
        scratch_shapes=SCRATCH + LEVEL_SCRATCH + COLUMN_SCRATCH * 2,
        compiler_params=params(),
        cost_estimate=cost(12, 24 << 20),
        name="products",
    )(core, second_way, gain, depth, depths, own, lam, *arrivals, fm, fo, am, ao, added)


SUB = QUARTER // LINE
PACKED = 3 * SUB + 8
PARTS = [by_level(PACKED, GY)] * LINE
CARRIES = by_level(3 * SUB, GY)


def in_place_order(place, pieces, ordered):
    for slot, piece in enumerate(pieces):
        ordered[lax.rem(place[0] + slot, LINE)] = piece[0]


def factor_after(place, slots, level, f, j):
    slot = lax.rem(j - place[0] + LINE, LINE)
    values = [ref[2 * f + level] for ref in slots]
    return jnp.where(slot < 2, jnp.where(slot == 0, values[0], values[1]), jnp.where(slot == 2, values[2], values[3]))


def line_total_body(place, line, d0, d1, d2, d3, a0, a1, a2, a3, *rest):
    outs, ordered = rest[:LINE], rest[LINE]
    level = pl.program_id(0)
    in_place_order(place, (a0, a1, a2, a3), ordered)
    rows = lax.broadcasted_iota(jnp.int32, (8, GY), 0)
    plane = jnp.zeros((8, GY), F32)
    for f in range(3):
        factors = [factor_after(place, (d0, d1, d2, d3), level, f, j) for j in range(LINE)]
        plane = jnp.where(rows == f, (factors[0] * factors[1]) * (factors[2] * factors[3]), plane)
        for slot, out in enumerate(outs):
            r = pl.multiple_of(lax.rem(line[0] + slot, LINE) * SUB, SUB)
            value = ordered[0, f, pl.ds(r, SUB), :]
            for j in range(1, LINE):
                value = factors[j] * value + ordered[j, f, pl.ds(r, SUB), :]
            out[0, SUB * f : SUB * f + SUB, :] = value
    for out in outs:
        out[0, 3 * SUB :, :] = plane


ORDERED = pltpu.VMEM((LINE, 3, QUARTER, GY), F32)


def line_total(place, line, factors, pieces):
    return pl.pallas_call(
        line_total_body,
        grid=(2,),
        in_specs=[SMEM] * (2 + LINE) + PIECES,
        out_specs=PARTS,
        out_shape=[shape(2, PACKED, GY)] * LINE,
        scratch_shapes=[ORDERED],
        compiler_params=params(),
        cost_estimate=cost(1, 2 << 20),
        name="line_total",
    )(place, line, *factors, *pieces)


def lines_onward(carry, ordered, f):
    out = [carry]
    for j in range(LINE):
        factor = ordered[j, 3 * SUB + f : 3 * SUB + f + 1, :]
        out.append(factor * out[-1] + ordered[j, SUB * f : SUB * f + SUB, :])
    return out


def put_in_order(line, parts, ordered):
    for slot, part in enumerate(parts):
        ordered[lax.rem(line[0] + slot, LINE)] = part[0]


def half_total_body(line, a0, a1, a2, a3, out, ordered):
    put_in_order(line, (a0, a1, a2, a3), ordered)
    for f in range(3):
        out[0, SUB * f : SUB * f + SUB, :] = lines_onward(jnp.zeros((SUB, GY), F32), ordered, f)[LINE]


def half_total(line, parts):
    return pl.pallas_call(
        half_total_body,
        grid=(2,),
        in_specs=[SMEM] + PARTS,
        out_specs=CARRIES,
        out_shape=shape(2, 3 * SUB, GY),
        scratch_shapes=[pltpu.VMEM((LINE, PACKED, GY), F32)],
        compiler_params=params(),
        cost_estimate=cost(1, 1 << 20),
        name="half_total",
    )(line, *parts)


def line_carries_body(line, carried, a0, a1, a2, a3, o0, o1, o2, o3, ordered, carries):
    put_in_order(line, (a0, a1, a2, a3), ordered)
    for f in range(3):
        rows = slice(SUB * f, SUB * f + SUB)
        for j, value in enumerate(lines_onward(carried[0, rows, :], ordered, f)[:LINE]):
            carries[j, rows, :] = value
    for slot, out in enumerate((o0, o1, o2, o3)):
        out[0] = carries[lax.rem(line[0] + slot, LINE)]


def line_carries(line, carried, parts):
    return pl.pallas_call(
        line_carries_body,
        grid=(2,),
        in_specs=[SMEM, CARRIES] + PARTS,
        out_specs=[CARRIES] * LINE,
        out_shape=[shape(2, 3 * SUB, GY)] * LINE,
        scratch_shapes=[pltpu.VMEM((LINE, PACKED, GY), F32), pltpu.VMEM((LINE, 3 * SUB, GY), F32)],
        compiler_params=params(),
        cost_estimate=cost(1, 1 << 20),
        name="line_carries",
    )(line, carried, *parts)


def spread_body(place, line, d0, d1, d2, d3, c0, c1, c2, c3, a0, a1, a2, a3, o0, o1, o2, o3, ordered):
    level = pl.program_id(0)
    in_place_order(place, (a0, a1, a2, a3), ordered)
    for f in range(3):
        factors = [factor_after(place, (d0, d1, d2, d3), level, f, j) for j in range(LINE)]
        for part, carried in enumerate((c0, c1, c2, c3)):
            r = pl.multiple_of(lax.rem(line[0] + part, LINE) * SUB, SUB)
            value = carried[0, SUB * f : SUB * f + SUB, :]
            for j in range(LINE):
                term = ordered[j, f, pl.ds(r, SUB), :]
                ordered[j, f, pl.ds(r, SUB), :] = value
                value = factors[j] * value + term
    for slot, out in enumerate((o0, o1, o2, o3)):
        out[0] = ordered[lax.rem(place[0] + slot, LINE)]


def spread(place, line, factors, carried, pieces):
    return pl.pallas_call(
        spread_body,
        grid=(2,),
        in_specs=[SMEM] * (2 + LINE) + [CARRIES] * LINE + PIECES,
        out_specs=PIECES,
        out_shape=PIECE_SHAPES,
        scratch_shapes=[ORDERED],
        compiler_params=params(),
        cost_estimate=cost(1, 4 << 20),
        name="spread",
    )(place, line, *factors, *carried, *pieces)


def finish_body(place, own, a0, a1, a2, a3, out):
    for slot, part in enumerate((a0, a1, a2, a3)):
        rows = pl.ds(pl.multiple_of(lax.rem(place[0] + slot, LINE) * QUARTER, QUARTER), QUARTER)
        for f in range(3):
            out[f, 0, rows, :] = own[f, 0, rows, :] + part[0, f]


def finish(place, own, parts):
    return pl.pallas_call(
        finish_body,
        grid=(2,),
        in_specs=[SMEM, STATE] + PIECES,
        out_specs=STATE,
        out_shape=shape(3, 2, GX, GY),
        compiler_params=params(),
        cost_estimate=cost(5, 9 << 20),
        name="finish",
    )(place, own, *parts)


def along(axis, distance):
    size = lax.axis_size(axis)
    return [(i, i + distance) for i in range(size) if 0 <= i + distance < size]


def swap(array, bit):
    return lax.ppermute(array, "lev", [(i, i ^ bit) for i in range(lax.axis_size("lev"))])


def around(array, distance):
    size = lax.axis_size("tm")
    return lax.ppermute(
        array, "tm", [(i, i - i % LINE + (i % LINE + distance) % LINE) for i in range(size)]
    )


def sideways(array, distance):
    size, four = lax.axis_size("tm"), LINE * LINE
    return lax.ppermute(
        array, "tm", [(i, i - i % four + (i % four + LINE * distance) % four) for i in range(size)]
    )


def to_second_half(array):
    half = lax.axis_size("tm") // 2
    return lax.ppermute(array, "tm", [(i, i + half) for i in range(half)])


def shards(
    increment, multiplier, error_var, obs_cell, obs_dual, obs_var, level_gain, mean_depth, chain_decay
):
    x, lam, ev = increment[0], multiplier[0], error_var[0]
    lev = lax.axis_index("lev")
    core, ylo = lev % 2, lev // 2
    core_arr = core.astype(jnp.int32).reshape(1)
    slab = lax.axis_index("tm")
    place = (slab % LINE).astype(jnp.int32).reshape(1)

    def exchanged(pieces, move=around):
        out = [pieces[0]]
        for slot, distance in ((3, -1), (2, 2), (1, 1)):
            out.append(move(pieces[slot], distance))
        return out

    own = lax.ppermute(chain_decay[0].reshape(6), "tm", along("tm", -1))
    size = lax.axis_size("tm")
    mid, half_ring = size // 2, lambda d: [(i, i - i % mid + (i % mid + d) % mid) for i in range(size)]
    arrivals = []
    for array, step in ((x, 1), (lam, -1)):
        ends = (0, mid) if step > 0 else (mid - 1, size - 1)
        first = lax.ppermute(array[:SENT_FIRST], "tm", half_ring(step))
        first_2 = lax.ppermute(first, "tm", [ends if step > 0 else ends[::-1]])
        last = around(array[SENT_FIRST:], step)
        hops = [(i, i + LINE * step) for i in range(0 if step > 0 else LINE - 1, size, LINE)]
        last_2 = lax.ppermute(last, "tm", [(i, j) for i, j in hops if 0 <= j < size])
        arrivals += [first, first_2, last, last_2]
    second_way = jnp.stack(
        [slab % mid == 0, slab % LINE == 0, slab % mid == mid - 1, slab % LINE == LINE - 1]
    ).astype(jnp.int32)
    here = exchanged([own] * LINE)
    fm, ft = partials(forward_partials_body, core_arr, level_gain, mean_depth, x, SCRATCH)
    fm = fm + swap(ft, 1)
    fm = fm + swap(fm, 2)
    fo = swap(fm, 1)
    am, at = partials(adjoint_partials_body, core_arr, level_gain, mean_depth, lam, SCRATCH + LEVEL_SCRATCH)
    am = am + swap(at, 1)
    am = am + swap(am, 2)

    own_rows, *terms = chain_terms(
        core_arr, place, level_gain, mean_depth, own, x, lam, ev, fm, fo
    )
    cells, duals, terms[0] = lax.optimization_barrier((obs_cell[0], obs_dual[0], terms[0]))
    rows, cols = cells // GY, cells % GY
    level = lax.broadcasted_iota(jnp.int32, rows.shape, 0)
    obs_product = obs_var[0] * duals + x[jnp.zeros_like(level), level, rows, cols]
    added = jnp.zeros(x[0].shape, F32).at[level, rows, cols].add(duals)

    line = (slab // LINE % LINE).astype(jnp.int32).reshape(1)
    pieces = exchanged(terms)
    pieces[0], added = lax.optimization_barrier((pieces[0], added))
    sums = line_total(place, line, here, pieces)
    sums = exchanged(sums, sideways)
    carried = to_second_half(half_total(line, sums))
    carries = line_carries(line, carried, sums)
    carries = exchanged(carries, sideways)
    parts = spread(place, line, here, carries, pieces)
    parts = exchanged(parts)
    chain = finish(place, own_rows, parts)

    quarter = HALF // 2
    fq = lax.ppermute(
        lax.dynamic_slice_in_dim(fm, ylo * quarter, quarter, 1), "tm", along("tm", 1)
    )
    aq = lax.ppermute(lax.dynamic_slice_in_dim(am, ylo * quarter, quarter, 1), "tm", along("tm", -1))
    q = jnp.concatenate([fq, aq])
    qo = swap(q, 2)
    half = jnp.where(ylo == 0, jnp.concatenate([q, qo], 1), jnp.concatenate([qo, q], 1))
    other = swap(half, 1)

    dual, block = products(
        core_arr, second_way, level_gain, mean_depth, fm, own_rows, lam, arrivals,
        half, other, half, other, added,
    )
    return dual[None], obs_product[None], block[None], chain[None]


def solution(mesh):
    state = P("tm", None, "lev", None, None)
    obs = P("tm", "lev", None)

    return jax.shard_map(
        shards,
        mesh=mesh,
        in_specs=(state, state, state, obs, obs, obs, P("lev"), P("lev"), P("tm", None, "lev")),
        out_specs=(state, obs, state, state),
        check_vma=False,
    )
```

profile of v0, /device:TPU:16, one launch (start us, length us, event | category | flops | bytes accessed | tf_op | source)
XLA Modules:
  0.0 319.6 jit_solution(8762006234229748847)
XLA Ops:
  0.6 3.7 %shard_map.120 = (f32[2,136,512]{2,1,0:T(8,128)}, f32[2,136,512]{2,1,0:T(8,128)}) custom-call(s32[1]{0:T(128)} %bitcast.core, f32[2]{0:T(128)} %gain.7, f32[2]{0:T(128)} %depth.7, f32[3,2,256,512]{3,2,1,0:T(8,128)} %bitcast.49), custom_call_target="tpu_custom_call" | custom-call | flops 16000000 | bytes 4194304 | tf_op jit(solution)/shard_map/pallas_call | solution.py:199
  9.1 13.4 %collective-permute-done.1 = f32[2,136,512]{2,1,0:T(8,128)S(1)} collective-permute-done((f32[2,136,512]{2,1,0:T(8,128)S(1)}, f32[2,136,512]{2,1,0:T(8,128)S(1)}, u32[]{:S(2)}, u32[]{:S(2)}) %collective-permute-start.1) | collective-permute-done | bytes 557088 | tf_op jit(solution)/shard_map/ppermute | solution.py:540
  23.5 7.9 %collective-permute-start.2 = (f32[6]{0:T(128)S(1)}, f32[6]{0:T(128)S(1)}, u32[]{:S(2)}, u32[]{:S(2)}) collective-permute-start(f32[6]{0:T(128)S(1)} %reshape_squeeze.3), channel_id=1, source_target_pairs={{4,0},{8,4},{12,8},{16,12},{20,16},{24,20},{28,24},{32,28},{36,32}... | collective-permute-start | bytes 80 | tf_op jit(solution)/shard_map/ppermute | solution.py:578
  33.5 8.1 %chain_terms.1 = (f32[3,2,256,512]{3,2,1,0:T(8,128)}, f32[2,3,64,512]{3,2,1,0:T(8,128)}, f32[2,3,64,512]{3,2,1,0:T(8,128)}, f32[2,3,64,512]{3,2,1,0:T(8,128)}, f32[2,3,64,512]{3,2,1,0:T(8,128)}) custom-call(s32[1]{0:T(128)} %bitcast.core, s32[1]{0:T(128)} %bitcast.6.place, f32[2]{0:T(128)} %gain.7, f32[2]{0:T(128)} %depth.7, f32[6]{0:T(128)} %copy-done.10, ...), custom_call_target="tpu_custom_call" | custom-call | flops 28000000 | bytes 16777216 | tf_op jit(solution)/shard_map/chain_terms/pallas_call | solution.py:297
  41.6 2.4 collective-permute-start.21
  44.0 4.8 %shard_map.121 = (f32[2,136,512]{2,1,0:T(8,128)}, f32[2,136,512]{2,1,0:T(8,128)}) custom-call(s32[1]{0:T(128)} %bitcast.core, f32[2]{0:T(128)} %gain.7, f32[2]{0:T(128)} %depth.7, f32[3,2,256,512]{3,2,1,0:T(8,128)} %bitcast.53), custom_call_target="tpu_custom_call" | custom-call | flops 16000000 | bytes 4194304 | tf_op jit(solution)/shard_map/pallas_call | solution.py:199
  48.9 3.2 %slice_bitcast_fusion.1 = f32[2,2,256,512]{3,2,1,0:T(8,128)} fusion(f32[1,3,2,256,512]{4,3,2,1,0:T(8,128)} %param.9), kind=kLoop, calls=%fused_computation.3 | loop fusion | bytes 4194304 | tf_op jit(solution)/shard_map/slice | solution.py:584
  52.3 4.1 %collective-permute-start.18 = (f32[6]{0:T(128)S(1)}, f32[6]{0:T(128)S(1)}, u32[]{:S(2)}, u32[]{:S(2)}) collective-permute-start(f32[6]{0:T(128)S(1)} %copy-done.11), channel_id=1, source_target_pairs={{0,12},{4,0},{8,4},{12,8},{16,28},{20,16},{24,20},{28,24},{32,44},... | collective-permute-start | bytes 80 | tf_op jit(solution)/shard_map/ppermute | solution.py:545
  56.4 4.6 %collective-permute-done.18.d1 = f32[6]{0:T(128)S(1)} collective-permute-done((f32[6]{0:T(128)S(1)}, f32[6]{0:T(128)S(1)}, u32[]{:S(2)}, u32[]{:S(2)}) %collective-permute-start.18) | collective-permute-done | bytes 56 | tf_op jit(solution)/shard_map/ppermute | solution.py:545
  61.0 38.8 %collective-permute-done.19.d2 = f32[6]{0:T(128)S(1)} collective-permute-done((f32[6]{0:T(128)S(1)}, f32[6]{0:T(128)S(1)}, u32[]{:S(2)}, u32[]{:S(2)}) %collective-permute-start.19) | collective-permute-done | bytes 56 | tf_op jit(solution)/shard_map/ppermute | solution.py:545
  104.2 3.0 collective-permute-start.8
  109.7 6.2 %scatter_custom_fusion = f32[262144]{0:T(1024)S(1)} fusion(s32[1024]{0:T(1024)S(1)} %bitcast.61, f32[1024]{0:T(1024)S(1)} %bitcast.62, f32[]{:T(128)} %constant.108.clone.1), kind=kCustom, calls=%fused_computation.7 | custom fusion | flops 1024 | bytes 1048580
  117.1 5.0 %collective-permute-done.22.a2 = f32[2,3,64,512]{3,2,1,0:T(8,128)} collective-permute-done((f32[2,3,64,512]{3,2,1,0:T(8,128)}, f32[2,3,64,512]{3,2,1,0:T(8,128)}, u32[]{:S(2)}, u32[]{:S(2)}) %collective-permute-start.22) | collective-permute-done | bytes 786464 | tf_op jit(solution)/shard_map/ppermute | solution.py:545
  122.1 15.4 %collective-permute-done.23.a3 = f32[2,3,64,512]{3,2,1,0:T(8,128)} collective-permute-done((f32[2,3,64,512]{3,2,1,0:T(8,128)S(1)}, f32[2,3,64,512]{3,2,1,0:T(8,128)}, u32[]{:S(2)}, u32[]{:S(2)}) %collective-permute-start.23) | collective-permute-done | bytes 786464 | tf_op jit(solution)/shard_map/ppermute | solution.py:545
  137.5 2.8 line_total.1
  141.6 2.5 collective-permute-start.25
  149.0 11.6 %collective-permute-done.24.a1 = f32[2,56,512]{2,1,0:T(8,128)} collective-permute-done((f32[2,56,512]{2,1,0:T(8,128)}, f32[2,56,512]{2,1,0:T(8,128)}, u32[]{:S(2)}, u32[]{:S(2)}) %collective-permute-start.24) | collective-permute-done | bytes 229408 | tf_op jit(solution)/shard_map/ppermute | solution.py:552
  160.6 3.9 %collective-permute-start.15 = (f32[2,64,512]{2,1,0:T(8,128)}, f32[2,64,512]{2,1,0:T(8,128)}, u32[]{:S(2)}, u32[]{:S(2)}) collective-permute-start(f32[2,64,512]{2,1,0:T(8,128)} %dynamic-slice_add_fusion), channel_id=1, source_target_pairs={{4,0},{8,4},{12,8},{16,12},{20,16},{24,20},{28,24},{32,28},{36,32}... | collective-permute-start | bytes 786440 | tf_op jit(solution)/shard_map/ppermute | solution.py:627
  170.0 17.5 %collective-permute-done.15 = f32[2,64,512]{2,1,0:T(8,128)} collective-permute-done((f32[2,64,512]{2,1,0:T(8,128)}, f32[2,64,512]{2,1,0:T(8,128)}, u32[]{:S(2)}, u32[]{:S(2)}) %collective-permute-start.15) | collective-permute-done | bytes 262176 | tf_op jit(solution)/shard_map/ppermute | solution.py:627
  193.3 18.2 %collective-permute-done.12 = f32[2,64,512]{2,1,0:T(8,128)} collective-permute-done((f32[2,64,512]{2,1,0:T(8,128)}, f32[2,64,512]{2,1,0:T(8,128)}, u32[]{:S(2)}, u32[]{:S(2)}) %collective-permute-start.12) | collective-permute-done | bytes 262176 | tf_op jit(solution)/shard_map/ppermute | solution.py:624
  217.2 3.4 %collective-permute-start.29 = (f32[2,48,512]{2,1,0:T(8,128)}, f32[2,48,512]{2,1,0:T(8,128)}, u32[]{:S(2)}, u32[]{:S(2)}) collective-permute-start(f32[2,48,512]{2,1,0:T(8,128)} %get-tuple-element.54), channel_id=1, source_target_pairs={{0,32},{4,36},{8,40},{12,44},{16,48},{20,52},{24,56},{28,60},{32,0... | collective-permute-start | bytes 589832 | tf_op jit(solution)/shard_map/ppermute | solution.py:552
  221.5 3.2 collective-permute-done.29.c2
  229.7 3.6 %spread.1 = (f32[2,3,64,512]{3,2,1,0:T(8,128)}, f32[2,3,64,512]{3,2,1,0:T(8,128)}, f32[2,3,64,512]{3,2,1,0:T(8,128)}, f32[2,3,64,512]{3,2,1,0:T(8,128)}) custom-call(s32[1]{0:T(128)} %bitcast.6.place, s32[1]{0:T(128)} %bitcast.21.line, f32[6]{0:T(128)} %copy-done.10, f32[6]{0:T(128)} %copy-done.13, f32[6]{0:T(128)} %copy-done.14, f32[6]{0:T(128)} %copy-done.15, ...), custom_call_target="tpu_custom_call" | custom-call | flops 4000000 | bytes 4194304 | tf_op jit(solution)/shard_map/spread/pallas_call | solution.py:501
  233.5 4.5 %collective-permute-start.32 = (f32[2,3,64,512]{3,2,1,0:T(8,128)}, f32[2,3,64,512]{3,2,1,0:T(8,128)S(1)}, u32[]{:S(2)}, u32[]{:S(2)}) collective-permute-start(f32[2,3,64,512]{3,2,1,0:T(8,128)} %get-tuple-element.58), channel_id=1, source_target_pairs={{0,8},{4,12},{8,0},{12,4},{16,24},{20,28},{24,16},{28,20},{32,40},... | collective-permute-start | bytes 2359304 | tf_op jit(solution)/shard_map/ppermute | solution.py:545
  238.0 2.7 maximum_select_fusion.fm.am
  240.8 13.8 %collective-permute-done.31.a1 = f32[2,3,64,512]{3,2,1,0:T(8,128)S(1)} collective-permute-done((f32[2,3,64,512]{3,2,1,0:T(8,128)}, f32[2,3,64,512]{3,2,1,0:T(8,128)S(1)}, u32[]{:S(2)}, u32[]{:S(2)}) %collective-permute-start.31) | collective-permute-done | bytes 786464 | tf_op jit(solution)/shard_map/ppermute | solution.py:545
  256.6 2.8 collective-permute-start.7
  259.5 6.5 %collective-permute-done.33.a3 = f32[2,3,64,512]{3,2,1,0:T(8,128)S(1)} collective-permute-done((f32[2,3,64,512]{3,2,1,0:T(8,128)}, f32[2,3,64,512]{3,2,1,0:T(8,128)S(1)}, u32[]{:S(2)}, u32[]{:S(2)}) %collective-permute-start.33) | collective-permute-done | bytes 786464 | tf_op jit(solution)/shard_map/ppermute | solution.py:545
  267.5 16.0 %gather_fusion = f32[1024]{0:T(1024)S(1)} fusion(f32[3,2,256,512]{3,2,1,0:T(8,128)} %bitcast.51, s32[1024]{0:T(1024)S(1)} %bitcast.48), kind=kCustom, calls=%fused_computation | custom fusion | bytes 24576 | tf_op jit(solution)/shard_map/gather | solution.py:608
  284.1 4.1 %finish.1 = f32[3,2,256,512]{3,2,1,0:T(8,128)} custom-call(s32[1]{0:T(128)} %bitcast.6.place, f32[3,2,256,512]{3,2,1,0:T(8,128)} %get-tuple-element.34.own, f32[2,3,64,512]{3,2,1,0:T(8,128)} %get-tuple-element.56.a0, f32[2,3,64,512]{3,2,1,0:T(8,128)} %copy-done.2, f32[2,3,64,512]{3,2,1,0:T(8,128)} %copy-done.3, f32[2,3,64,512]{3,2,1,0:T(8,128)} %copy-done.4), custom_call_target="tpu_custom_call" | custom-call | flops 20000000 | bytes 9437184 | tf_op jit(solution)/shard_map/finish/pallas_call | solution.py:522
  288.2 19.0 %collective-permute-done.5.xr2 = f32[2,2,256,512]{3,2,1,0:T(8,128)} collective-permute-done((f32[2,2,256,512]{3,2,1,0:T(8,128)}, f32[2,2,256,512]{3,2,1,0:T(8,128)}, u32[]{:S(2)}, u32[]{:S(2)}) %collective-permute-start.5) | collective-permute-done | bytes 2097184 | tf_op jit(solution)/shard_map/ppermute | solution.py:585
  307.2 12.3 %products.1 = (f32[3,2,256,512]{3,2,1,0:T(8,128)}, f32[3,2,256,512]{3,2,1,0:T(8,128)}) custom-call(s32[1]{0:T(128)} %bitcast.core, s32[4]{0:T(128)} %add_convert_fusion.second_way, f32[2]{0:T(128)} %gain.7, f32[2]{0:T(128)} %depth.7, f32[2,136,512]{2,1,0:T(8,128)} %copy-done.1, f32[3,2,256,512]{3,2,1,0:T(8,128)} %get-tuple-element.34.own, ...), custom_call_target="tpu_custom_call" | custom-call | flops 48000000 | bytes 25165824 | tf_op jit(solution)/shard_map/products/pallas_call | solution.py:356
  (114 shorter events, 49.3 us)
Async XLA Ops:
  7.7 14.7 %collective-permute-start.1 = (f32[2,136,512]{2,1,0:T(8,128)S(1)}, f32[2,136,512]{2,1,0:T(8,128)S(1)}, u32[]{:S(2)}, u32[]{:S(2)}) collective-permute-start(f32[2,136,512]{2,1,0:T(8,128)S(1)} %add.60), channel_id=1, source_target_pairs={{0,2},{1,3},{2,0},{3,1},{4,6},{5,7},{6,4},{7,5},{8,10},{9,11},{10,... | collective-permute-start | bytes 1671176 | tf_op jit(solution)/shard_map/ppermute | solution.py:540
  23.4 9.4 %collective-permute-start.3 = (f32[2,136,512]{2,1,0:T(8,128)S(1)}, f32[2,136,512]{2,1,0:T(8,128)S(1)}, u32[]{:S(2)}, u32[]{:S(2)}) collective-permute-start(f32[2,136,512]{2,1,0:T(8,128)S(1)} %add.61.mine.depths), channel_id=1, source_target_pairs={{0,1},{1,0},{2,3},{3,2},{4,5},{5,4},{6,7},{7,6},{8,9},{9,8},{10,11... | collective-permute-start | bytes 1671176 | tf_op jit(solution)/shard_map/ppermute | solution.py:540
  23.5 9.2 %collective-permute-start.2 = (f32[6]{0:T(128)S(1)}, f32[6]{0:T(128)S(1)}, u32[]{:S(2)}, u32[]{:S(2)}) collective-permute-start(f32[6]{0:T(128)S(1)} %reshape_squeeze.3), channel_id=1, source_target_pairs={{4,0},{8,4},{12,8},{16,12},{20,16},{24,20},{28,24},{32,28},{36,32}... | collective-permute-start | bytes 80 | tf_op jit(solution)/shard_map/ppermute | solution.py:578
  41.6 66.5 %collective-permute-start.21 = (f32[2,3,64,512]{3,2,1,0:T(8,128)}, f32[2,3,64,512]{3,2,1,0:T(8,128)}, u32[]{:S(2)}, u32[]{:S(2)}) collective-permute-start(f32[2,3,64,512]{3,2,1,0:T(8,128)} %get-tuple-element.45), channel_id=1, source_target_pairs={{0,12},{4,0},{8,4},{12,8},{16,28},{20,16},{24,20},{28,24},{32,44},... | collective-permute-start | bytes 2359304 | tf_op jit(solution)/shard_map/ppermute | solution.py:545
  48.9 55.3 %collective-permute-start.13 = (f32[2,136,512]{2,1,0:T(8,128)}, f32[2,136,512]{2,1,0:T(8,128)S(1)}, u32[]{:S(2)}, u32[]{:S(2)}) collective-permute-start(f32[2,136,512]{2,1,0:T(8,128)} %get-tuple-element.36), channel_id=1, source_target_pairs={{0,1},{1,0},{2,3},{3,2},{4,5},{5,4},{6,7},{7,6},{8,9},{9,8},{10,11... | collective-permute-start | bytes 1671176 | tf_op jit(solution)/shard_map/ppermute | solution.py:540
  52.2 163.7 %collective-permute-start.4 = (f32[2,2,256,512]{3,2,1,0:T(8,128)}, f32[2,2,256,512]{3,2,1,0:T(8,128)}, u32[]{:S(2)}, u32[]{:S(2)}) collective-permute-start(f32[2,2,256,512]{3,2,1,0:T(8,128)} %slice_bitcast_fusion.1), channel_id=1, source_target_pairs={{0,4},{4,8},{8,12},{12,16},{16,20},{20,24},{24,28},{28,32},{32,36}... | collective-permute-start | bytes 6291464 | tf_op jit(solution)/shard_map/ppermute | solution.py:584
  52.3 8.7 %collective-permute-start.18 = (f32[6]{0:T(128)S(1)}, f32[6]{0:T(128)S(1)}, u32[]{:S(2)}, u32[]{:S(2)}) collective-permute-start(f32[6]{0:T(128)S(1)} %copy-done.11), channel_id=1, source_target_pairs={{0,12},{4,0},{8,4},{12,8},{16,28},{20,16},{24,20},{28,24},{32,44},... | collective-permute-start | bytes 80 | tf_op jit(solution)/shard_map/ppermute | solution.py:545
  56.4 43.4 %collective-permute-start.19 = (f32[6]{0:T(128)S(1)}, f32[6]{0:T(128)S(1)}, u32[]{:S(2)}, u32[]{:S(2)}) collective-permute-start(f32[6]{0:T(128)S(1)} %copy-done.11), channel_id=1, source_target_pairs={{0,8},{4,12},{8,0},{12,4},{16,24},{20,28},{24,16},{28,20},{32,40},... | collective-permute-start | bytes 80 | tf_op jit(solution)/shard_map/ppermute | solution.py:545
  61.0 41.2 %collective-permute-start.20 = (f32[6]{0:T(128)S(1)}, f32[6]{0:T(128)S(1)}, u32[]{:S(2)}, u32[]{:S(2)}) collective-permute-start(f32[6]{0:T(128)S(1)} %copy-done.11), channel_id=1, source_target_pairs={{0,4},{4,8},{8,12},{12,0},{16,20},{20,24},{24,28},{28,16},{32,36},... | collective-permute-start | bytes 80 | tf_op jit(solution)/shard_map/ppermute | solution.py:545
  99.9 22.3 %collective-permute-start.22 = (f32[2,3,64,512]{3,2,1,0:T(8,128)}, f32[2,3,64,512]{3,2,1,0:T(8,128)}, u32[]{:S(2)}, u32[]{:S(2)}) collective-permute-start(f32[2,3,64,512]{3,2,1,0:T(8,128)} %get-tuple-element.46), channel_id=1, source_target_pairs={{0,8},{4,12},{8,0},{12,4},{16,24},{20,28},{24,16},{28,20},{32,40},... | collective-permute-start | bytes 2359304 | tf_op jit(solution)/shard_map/ppermute | solution.py:545
  102.7 34.8 %collective-permute-start.23 = (f32[2,3,64,512]{3,2,1,0:T(8,128)S(1)}, f32[2,3,64,512]{3,2,1,0:T(8,128)}, u32[]{:S(2)}, u32[]{:S(2)}) collective-permute-start(f32[2,3,64,512]{3,2,1,0:T(8,128)S(1)} %copy-done.19), channel_id=1, source_target_pairs={{0,4},{4,8},{8,12},{12,0},{16,20},{20,24},{24,28},{28,16},{32,36},... | collective-permute-start | bytes 2359304 | tf_op jit(solution)/shard_map/ppermute | solution.py:545
  104.2 113.0 %collective-permute-start.8 = (f32[2,2,256,512]{3,2,1,0:T(8,128)}, f32[2,2,256,512]{3,2,1,0:T(8,128)}, u32[]{:S(2)}, u32[]{:S(2)}) collective-permute-start(f32[2,2,256,512]{3,2,1,0:T(8,128)} %slice_bitcast_fusion), channel_id=1, source_target_pairs={{0,60},{4,0},{8,4},{12,8},{16,12},{20,16},{24,20},{28,24},{32,28},... | collective-permute-start | bytes 6291464 | tf_op jit(solution)/shard_map/ppermute | solution.py:584
  108.1 36.0 %collective-permute-start.14 = (f32[2,136,512]{2,1,0:T(8,128)}, f32[2,136,512]{2,1,0:T(8,128)}, u32[]{:S(2)}, u32[]{:S(2)}) collective-permute-start(f32[2,136,512]{2,1,0:T(8,128)} %add.63), channel_id=1, source_target_pairs={{0,2},{1,3},{2,0},{3,1},{4,6},{5,7},{6,4},{7,5},{8,10},{9,11},{10,... | collective-permute-start | bytes 1671176 | tf_op jit(solution)/shard_map/ppermute | solution.py:540
  140.3 20.3 %collective-permute-start.24 = (f32[2,56,512]{2,1,0:T(8,128)}, f32[2,56,512]{2,1,0:T(8,128)}, u32[]{:S(2)}, u32[]{:S(2)}) collective-permute-start(f32[2,56,512]{2,1,0:T(8,128)} %get-tuple-element.49), channel_id=1, source_target_pairs={{0,48},{4,52},{8,56},{12,60},{16,0},{20,4},{24,8},{28,12},{32,16},... | collective-permute-start | bytes 688136 | tf_op jit(solution)/shard_map/ppermute | solution.py:552
  141.6 19.0 %collective-permute-start.25 = (f32[2,56,512]{2,1,0:T(8,128)}, f32[2,56,512]{2,1,0:T(8,128)}, u32[]{:S(2)}, u32[]{:S(2)}) collective-permute-start(f32[2,56,512]{2,1,0:T(8,128)} %get-tuple-element.50), channel_id=1, source_target_pairs={{0,32},{4,36},{8,40},{12,44},{16,48},{20,52},{24,56},{28,60},{32,0... | collective-permute-start | bytes 688136 | tf_op jit(solution)/shard_map/ppermute | solution.py:552
  144.1 20.4 %collective-permute-start.26 = (f32[2,56,512]{2,1,0:T(8,128)}, f32[2,56,512]{2,1,0:T(8,128)}, u32[]{:S(2)}, u32[]{:S(2)}) collective-permute-start(f32[2,56,512]{2,1,0:T(8,128)} %get-tuple-element.51), channel_id=1, source_target_pairs={{0,16},{4,20},{8,24},{12,28},{16,32},{20,36},{24,40},{28,44},{32,4... | collective-permute-start | bytes 688136 | tf_op jit(solution)/shard_map/ppermute | solution.py:552
  160.6 72.8 %collective-permute-start.10 = (f32[1,2,256,512]{3,2,1,0:T(8,128)}, f32[1,2,256,512]{3,2,1,0:T(8,128)}, u32[]{:S(2)}, u32[]{:S(2)}) collective-permute-start(f32[1,2,256,512]{3,2,1,0:T(8,128)} %slice_bitcast_fusion.2), channel_id=1, source_target_pairs={{0,12},{4,0},{8,4},{12,8},{16,28},{20,16},{24,20},{28,24},{32,44},... | collective-permute-start | bytes 3145736 | tf_op jit(solution)/shard_map/ppermute | solution.py:545
  160.6 27.0 %collective-permute-start.15 = (f32[2,64,512]{2,1,0:T(8,128)}, f32[2,64,512]{2,1,0:T(8,128)}, u32[]{:S(2)}, u32[]{:S(2)}) collective-permute-start(f32[2,64,512]{2,1,0:T(8,128)} %dynamic-slice_add_fusion), channel_id=1, source_target_pairs={{4,0},{8,4},{12,8},{16,12},{20,16},{24,20},{28,24},{32,28},{36,32}... | collective-permute-start | bytes 786440 | tf_op jit(solution)/shard_map/ppermute | solution.py:627
  166.5 22.8 %collective-permute-start.27 = (f32[2,48,512]{2,1,0:T(8,128)}, f32[2,48,512]{2,1,0:T(8,128)}, u32[]{:S(2)}, u32[]{:S(2)}) collective-permute-start(f32[2,48,512]{2,1,0:T(8,128)} %half_total.1), channel_id=1, source_target_pairs={{0,64},{4,68},{8,72},{12,76},{16,80},{20,84},{24,88},{28,92},{32,9... | collective-permute-start | bytes 589832 | tf_op jit(solution)/shard_map/ppermute | solution.py:559
  187.6 45.9 %collective-permute-start.6 = (f32[1,2,256,512]{3,2,1,0:T(8,128)}, f32[1,2,256,512]{3,2,1,0:T(8,128)}, u32[]{:S(2)}, u32[]{:S(2)}) collective-permute-start(f32[1,2,256,512]{3,2,1,0:T(8,128)} %slice_bitcast_fusion.3), channel_id=1, source_target_pairs={{0,4},{4,8},{8,12},{12,0},{16,20},{20,24},{24,28},{28,16},{32,36},... | collective-permute-start | bytes 3145736 | tf_op jit(solution)/shard_map/ppermute | solution.py:545
  189.3 22.2 %collective-permute-start.12 = (f32[2,64,512]{2,1,0:T(8,128)}, f32[2,64,512]{2,1,0:T(8,128)}, u32[]{:S(2)}, u32[]{:S(2)}) collective-permute-start(f32[2,64,512]{2,1,0:T(8,128)} %constant_dynamic-slice_fusion), channel_id=1, source_target_pairs={{0,4},{4,8},{8,12},{12,16},{16,20},{20,24},{24,28},{28,32},{32,36}... | collective-permute-start | bytes 786440 | tf_op jit(solution)/shard_map/ppermute | solution.py:624
  211.5 9.1 %collective-permute-start.28 = (f32[2,48,512]{2,1,0:T(8,128)}, f32[2,48,512]{2,1,0:T(8,128)}, u32[]{:S(2)}, u32[]{:S(2)}) collective-permute-start(f32[2,48,512]{2,1,0:T(8,128)} %get-tuple-element.53), channel_id=1, source_target_pairs={{0,48},{4,52},{8,56},{12,60},{16,0},{20,4},{24,8},{28,12},{32,16},... | collective-permute-start | bytes 589832 | tf_op jit(solution)/shard_map/ppermute | solution.py:552
  215.9 22.1 %collective-permute-start.16 = (f32[4,64,512]{2,1,0:T(8,128)}, f32[4,64,512]{2,1,0:T(8,128)}, u32[]{:S(2)}, u32[]{:S(2)}) collective-permute-start(f32[4,64,512]{2,1,0:T(8,128)} %constant_dynamic-update-slice_fusion), channel_id=1, source_target_pairs={{0,2},{1,3},{2,0},{3,1},{4,6},{5,7},{6,4},{7,5},{8,10},{9,11},{10,... | collective-permute-start | bytes 1572872 | tf_op jit(solution)/shard_map/ppermute | solution.py:540
  217.2 7.5 %collective-permute-start.29 = (f32[2,48,512]{2,1,0:T(8,128)}, f32[2,48,512]{2,1,0:T(8,128)}, u32[]{:S(2)}, u32[]{:S(2)}) collective-permute-start(f32[2,48,512]{2,1,0:T(8,128)} %get-tuple-element.54), channel_id=1, source_target_pairs={{0,32},{4,36},{8,40},{12,44},{16,48},{20,52},{24,56},{28,60},{32,0... | collective-permute-start | bytes 589832 | tf_op jit(solution)/shard_map/ppermute | solution.py:552
  224.7 82.5 %collective-permute-start.5 = (f32[2,2,256,512]{3,2,1,0:T(8,128)}, f32[2,2,256,512]{3,2,1,0:T(8,128)}, u32[]{:S(2)}, u32[]{:S(2)}) collective-permute-start(f32[2,2,256,512]{3,2,1,0:T(8,128)} %collective-permute-done.4.xr), channel_id=1, source_target_pairs={{0,64},{1,65},{2,66},{3,67}} | collective-permute-start | bytes 6291464 | tf_op jit(solution)/shard_map/ppermute | solution.py:585
  227.8 79.4 %collective-permute-start.9 = (f32[2,2,256,512]{3,2,1,0:T(8,128)}, f32[2,2,256,512]{3,2,1,0:T(8,128)}, u32[]{:S(2)}, u32[]{:S(2)}) collective-permute-start(f32[2,2,256,512]{3,2,1,0:T(8,128)} %collective-permute-done.8.lr), channel_id=1, source_target_pairs={{124,60},{125,61},{126,62},{127,63}} | collective-permute-start | bytes 6291464 | tf_op jit(solution)/shard_map/ppermute | solution.py:585
  233.4 21.2 %collective-permute-start.31 = (f32[2,3,64,512]{3,2,1,0:T(8,128)}, f32[2,3,64,512]{3,2,1,0:T(8,128)S(1)}, u32[]{:S(2)}, u32[]{:S(2)}) collective-permute-start(f32[2,3,64,512]{3,2,1,0:T(8,128)} %get-tuple-element.57), channel_id=1, source_target_pairs={{0,12},{4,0},{8,4},{12,8},{16,28},{20,16},{24,20},{28,24},{32,44},... | collective-permute-start | bytes 2359304 | tf_op jit(solution)/shard_map/ppermute | solution.py:545
  233.5 23.1 %collective-permute-start.32 = (f32[2,3,64,512]{3,2,1,0:T(8,128)}, f32[2,3,64,512]{3,2,1,0:T(8,128)S(1)}, u32[]{:S(2)}, u32[]{:S(2)}) collective-permute-start(f32[2,3,64,512]{3,2,1,0:T(8,128)} %get-tuple-element.58), channel_id=1, source_target_pairs={{0,8},{4,12},{8,0},{12,4},{16,24},{20,28},{24,16},{28,20},{32,40},... | collective-permute-start | bytes 2359304 | tf_op jit(solution)/shard_map/ppermute | solution.py:545
  238.0 28.0 %collective-permute-start.33 = (f32[2,3,64,512]{3,2,1,0:T(8,128)}, f32[2,3,64,512]{3,2,1,0:T(8,128)S(1)}, u32[]{:S(2)}, u32[]{:S(2)}) collective-permute-start(f32[2,3,64,512]{3,2,1,0:T(8,128)} %get-tuple-element.59), channel_id=1, source_target_pairs={{0,4},{4,8},{8,12},{12,0},{16,20},{20,24},{24,28},{28,16},{32,36},... | collective-permute-start | bytes 2359304 | tf_op jit(solution)/shard_map/ppermute | solution.py:545
  254.6 33.6 %collective-permute-start.11 = (f32[1,2,256,512]{3,2,1,0:T(8,128)}, f32[1,2,256,512]{3,2,1,0:T(8,128)}, u32[]{:S(2)}, u32[]{:S(2)}) collective-permute-start(f32[1,2,256,512]{3,2,1,0:T(8,128)} %collective-permute-done.10.lv), channel_id=1, source_target_pairs={{28,12},{44,28},{60,44},{76,60},{92,76},{108,92},{124,108},{29,13}... | collective-permute-start | bytes 3145736 | tf_op jit(solution)/shard_map/ppermute | solution.py:588
  256.6 31.6 %collective-permute-start.7 = (f32[1,2,256,512]{3,2,1,0:T(8,128)}, f32[1,2,256,512]{3,2,1,0:T(8,128)}, u32[]{:S(2)}, u32[]{:S(2)}) collective-permute-start(f32[1,2,256,512]{3,2,1,0:T(8,128)} %collective-permute-done.6.xv), channel_id=1, source_target_pairs={{0,16},{16,32},{32,48},{48,64},{64,80},{80,96},{96,112},{1,17},{17... | collective-permute-start | bytes 3145736 | tf_op jit(solution)/shard_map/ppermute | solution.py:588
  266.0 22.2 %collective-permute-start.17 = (f32[4,128,512]{2,1,0:T(8,128)}, f32[4,128,512]{2,1,0:T(8,128)}, u32[]{:S(2)}, u32[]{:S(2)}) collective-permute-start(f32[4,128,512]{2,1,0:T(8,128)} %maximum_select_fusion.fm.am), channel_id=1, source_target_pairs={{0,1},{1,0},{2,3},{3,2},{4,5},{5,4},{6,7},{7,6},{8,9},{9,8},{10,11... | collective-permute-start | bytes 3145736 | tf_op jit(solution)/shard_map/ppermute | solution.py:540
  (22 other events, 617.8 us)
where the time goes:
time: 321 us; the launch traced here: 320 us
  waiting for transfers between devices  173 us (54%)
  starting transfers between devices  53.4 us (17%)
  Pallas kernels  43.6 us (14%)
  local copies, waits for them, and re-layouts  33.8 us (11%)
  other arithmetic  15.1 us (5%)
    ppermute x11, waiting for transfers between devices, around(): lax.ppermute(array, 'tm', [(i, i - i % LINE + (i % LINE + distance) % LIN...  84.6 us
    ppermute x2, waiting for transfers between devices, shards(): first_2 = lax.ppermute(first, 'tm', [ends if step > 0 else ends[::-1]])  19 us
    ppermute x1, waiting for transfers between devices, shards(): lax.ppermute(lax.dynamic_slice_in_dim(fm, ylo * quarter, quarter, 1), 'tm...  18.2 us
    ppermute x1, waiting for transfers between devices, shards(): lax.ppermute(lax.dynamic_slice_in_dim(am, ylo * quarter, quarter, 1), 'tm...  17.5 us
    ppermute x6, waiting for transfers between devices, sideways(): lax.ppermute(array, 'tm', [(i, i - i % four + (i % four + LINE * distance...  16.6 us
    gather x2, local copies, waits for them, and re-layouts, shards(): x[jnp.zeros_like(level), level, rows, cols]  16 us
    ppermute x7, waiting for transfers between devices, swap(): lax.ppermute(array, 'lev', [(i, i ^ bit) for i in range(lax.axis_size('le...  15.6 us
    ppermute x11, starting transfers between devices, around(): lax.ppermute(array, 'tm', [(i, i - i % LINE + (i % LINE + distance) % LIN...  13.5 us
  transfers between devices with their start and end apart: 34, of which 16 were waited for; matrix products, arithmetic and copies ran while one was open for 14% of the time, Pallas kernels for 6%

commit v1 on v0

--- a/solution.py
+++ b/solution.py
@@ -605,7 +605,10 @@
     cells, duals, terms[0] = lax.optimization_barrier((obs_cell[0], obs_dual[0], terms[0]))
     rows, cols = cells // GY, cells % GY
     level = lax.broadcasted_iota(jnp.int32, rows.shape, 0)
-    obs_product = obs_var[0] * duals + x[jnp.zeros_like(level), level, rows, cols]
+    seen = []
+    for k in range(2):
+        seen.append(x[jnp.zeros_like(rows[k]), jnp.full_like(rows[k], k), rows[k], cols[k]])
+    obs_product = obs_var[0] * duals + jnp.stack(seen)
     added = jnp.zeros(x[0].shape, F32).at[level, rows, cols].add(duals)
 
     line = (slab // LINE % LINE).astype(jnp.int32).reshape(1)

time: 321 us -> 321 us (level)
    unnamed x5 -> x4, other arithmetic: 7.08 us -> 6.36 us
where the time goes in v1:
time: 321 us; the launch traced here: 320 us
  waiting for transfers between devices  174 us (54%)
  starting transfers between devices  53.3 us (17%)
  Pallas kernels  43.6 us (14%)
  local copies, waits for them, and re-layouts  32.5 us (10%)
  other arithmetic  15.6 us (5%)
    ppermute x11, waiting for transfers between devices, around(): lax.ppermute(array, 'tm', [(i, i - i % LINE + (i % LINE + distance) % LIN...  84 us
    ppermute x2, waiting for transfers between devices, shards(): first_2 = lax.ppermute(first, 'tm', [ends if step > 0 else ends[::-1]])  20.3 us
    ppermute x1, waiting for transfers between devices, shards(): lax.ppermute(lax.dynamic_slice_in_dim(fm, ylo * quarter, quarter, 1), 'tm...  18.1 us
    ppermute x1, waiting for transfers between devices, shards(): lax.ppermute(lax.dynamic_slice_in_dim(am, ylo * quarter, quarter, 1), 'tm...  17.5 us
    ppermute x6, waiting for transfers between devices, sideways(): lax.ppermute(array, 'tm', [(i, i - i % four + (i % four + LINE * distance...  16.8 us
    ppermute x7, waiting for transfers between devices, swap(): lax.ppermute(array, 'lev', [(i, i ^ bit) for i in range(lax.axis_size('le...  15.6 us
    gather x2, local copies, waits for them, and re-layouts, shards(): x[jnp.zeros_like(rows[k]), jnp.full_like(rows[k], k), rows[k], cols[k]]  14.6 us
    ppermute x11, starting transfers between devices, around(): lax.ppermute(array, 'tm', [(i, i - i % LINE + (i % LINE + distance) % LIN...  13.5 us
  transfers between devices with their start and end apart: 34, of which 16 were waited for; matrix products, arithmetic and copies ran while one was open for 14% of the time, Pallas kernels for 6%

profile of v1, /device:TPU:16, one launch (start us, length us, event | category | flops | bytes accessed | tf_op | source)
XLA Modules:
  0.0 319.8 jit_solution(15362312759968822522)
XLA Ops:
  0.6 3.7 %shard_map.120 = (f32[2,136,512]{2,1,0:T(8,128)}, f32[2,136,512]{2,1,0:T(8,128)}) custom-call(s32[1]{0:T(128)} %bitcast.core, f32[2]{0:T(128)} %gain.7, f32[2]{0:T(128)} %depth.7, f32[3,2,256,512]{3,2,1,0:T(8,128)} %bitcast.58), custom_call_target="tpu_custom_call" | custom-call | flops 16000000 | bytes 4194304 | tf_op jit(solution)/shard_map/pallas_call | solution.py:199
  9.1 13.4 %collective-permute-done.1 = f32[2,136,512]{2,1,0:T(8,128)S(1)} collective-permute-done((f32[2,136,512]{2,1,0:T(8,128)S(1)}, f32[2,136,512]{2,1,0:T(8,128)S(1)}, u32[]{:S(2)}, u32[]{:S(2)}) %collective-permute-start.1) | collective-permute-done | bytes 557088 | tf_op jit(solution)/shard_map/ppermute | solution.py:540
  23.5 7.9 %collective-permute-start.2 = (f32[6]{0:T(128)S(1)}, f32[6]{0:T(128)S(1)}, u32[]{:S(2)}, u32[]{:S(2)}) collective-permute-start(f32[6]{0:T(128)S(1)} %reshape_squeeze.3), channel_id=1, source_target_pairs={{4,0},{8,4},{12,8},{16,12},{20,16},{24,20},{28,24},{32,28},{36,32}... | collective-permute-start | bytes 80 | tf_op jit(solution)/shard_map/ppermute | solution.py:578
  33.5 8.1 %chain_terms.1 = (f32[3,2,256,512]{3,2,1,0:T(8,128)}, f32[2,3,64,512]{3,2,1,0:T(8,128)}, f32[2,3,64,512]{3,2,1,0:T(8,128)}, f32[2,3,64,512]{3,2,1,0:T(8,128)}, f32[2,3,64,512]{3,2,1,0:T(8,128)}) custom-call(s32[1]{0:T(128)} %bitcast.core, s32[1]{0:T(128)} %bitcast.6.place, f32[2]{0:T(128)} %gain.7, f32[2]{0:T(128)} %depth.7, f32[6]{0:T(128)} %copy-done.7, ...), custom_call_target="tpu_custom_call" | custom-call | flops 28000000 | bytes 16777216 | tf_op jit(solution)/shard_map/chain_terms/pallas_call | solution.py:297
  44.0 4.8 %shard_map.121 = (f32[2,136,512]{2,1,0:T(8,128)}, f32[2,136,512]{2,1,0:T(8,128)}) custom-call(s32[1]{0:T(128)} %bitcast.core, f32[2]{0:T(128)} %gain.7, f32[2]{0:T(128)} %depth.7, f32[3,2,256,512]{3,2,1,0:T(8,128)} %bitcast.63), custom_call_target="tpu_custom_call" | custom-call | flops 16000000 | bytes 4194304 | tf_op jit(solution)/shard_map/pallas_call | solution.py:199
  48.9 3.2 %slice_bitcast_fusion.1 = f32[2,2,256,512]{3,2,1,0:T(8,128)} fusion(f32[1,3,2,256,512]{4,3,2,1,0:T(8,128)} %param.9), kind=kLoop, calls=%fused_computation.4 | loop fusion | bytes 4194304 | tf_op jit(solution)/shard_map/slice | solution.py:584
  52.3 4.1 %collective-permute-start.18 = (f32[6]{0:T(128)S(1)}, f32[6]{0:T(128)S(1)}, u32[]{:S(2)}, u32[]{:S(2)}) collective-permute-start(f32[6]{0:T(128)S(1)} %copy-done.8), channel_id=1, source_target_pairs={{0,12},{4,0},{8,4},{12,8},{16,28},{20,16},{24,20},{28,24},{32,44},... | collective-permute-start | bytes 80 | tf_op jit(solution)/shard_map/ppermute | solution.py:545
  56.4 4.6 %collective-permute-done.18.d1 = f32[6]{0:T(128)S(1)} collective-permute-done((f32[6]{0:T(128)S(1)}, f32[6]{0:T(128)S(1)}, u32[]{:S(2)}, u32[]{:S(2)}) %collective-permute-start.18) | collective-permute-done | bytes 56 | tf_op jit(solution)/shard_map/ppermute | solution.py:545
  61.0 38.8 %collective-permute-done.19.d2 = f32[6]{0:T(128)S(1)} collective-permute-done((f32[6]{0:T(128)S(1)}, f32[6]{0:T(128)S(1)}, u32[]{:S(2)}, u32[]{:S(2)}) %collective-permute-start.19) | collective-permute-done | bytes 56 | tf_op jit(solution)/shard_map/ppermute | solution.py:545
  104.3 3.0 collective-permute-start.8
  110.4 6.2 %scatter_custom_fusion = f32[262144]{0:T(1024)S(1)} fusion(s32[1024]{0:T(1024)S(1)} %bitcast.74, f32[1024]{0:T(1024)S(1)} %bitcast.75, f32[]{:T(128)} %constant.113.clone.1), kind=kCustom, calls=%fused_computation.8 | custom fusion | flops 1024 | bytes 1048580
  117.7 4.4 %collective-permute-done.22.a2 = f32[2,3,64,512]{3,2,1,0:T(8,128)} collective-permute-done((f32[2,3,64,512]{3,2,1,0:T(8,128)}, f32[2,3,64,512]{3,2,1,0:T(8,128)}, u32[]{:S(2)}, u32[]{:S(2)}) %collective-permute-start.22) | collective-permute-done | bytes 786464 | tf_op jit(solution)/shard_map/ppermute | solution.py:545
  122.1 15.4 %collective-permute-done.23.a3 = f32[2,3,64,512]{3,2,1,0:T(8,128)} collective-permute-done((f32[2,3,64,512]{3,2,1,0:T(8,128)S(1)}, f32[2,3,64,512]{3,2,1,0:T(8,128)}, u32[]{:S(2)}, u32[]{:S(2)}) %collective-permute-start.23) | collective-permute-done | bytes 786464 | tf_op jit(solution)/shard_map/ppermute | solution.py:545
  137.5 2.8 line_total.1
  141.6 2.5 collective-permute-start.25
  149.0 11.6 %collective-permute-done.24.a1 = f32[2,56,512]{2,1,0:T(8,128)} collective-permute-done((f32[2,56,512]{2,1,0:T(8,128)}, f32[2,56,512]{2,1,0:T(8,128)}, u32[]{:S(2)}, u32[]{:S(2)}) %collective-permute-start.24) | collective-permute-done | bytes 229408 | tf_op jit(solution)/shard_map/ppermute | solution.py:552
  160.7 3.9 %collective-permute-start.15 = (f32[2,64,512]{2,1,0:T(8,128)}, f32[2,64,512]{2,1,0:T(8,128)}, u32[]{:S(2)}, u32[]{:S(2)}) collective-permute-start(f32[2,64,512]{2,1,0:T(8,128)} %dynamic-slice_add_fusion), channel_id=1, source_target_pairs={{4,0},{8,4},{12,8},{16,12},{20,16},{24,20},{28,24},{32,28},{36,32}... | collective-permute-start | bytes 786440 | tf_op jit(solution)/shard_map/ppermute | solution.py:630
  170.2 17.5 %collective-permute-done.15 = f32[2,64,512]{2,1,0:T(8,128)} collective-permute-done((f32[2,64,512]{2,1,0:T(8,128)}, f32[2,64,512]{2,1,0:T(8,128)}, u32[]{:S(2)}, u32[]{:S(2)}) %collective-permute-start.15) | collective-permute-done | bytes 262176 | tf_op jit(solution)/shard_map/ppermute | solution.py:630
  193.5 18.1 %collective-permute-done.12 = f32[2,64,512]{2,1,0:T(8,128)} collective-permute-done((f32[2,64,512]{2,1,0:T(8,128)}, f32[2,64,512]{2,1,0:T(8,128)}, u32[]{:S(2)}, u32[]{:S(2)}) %collective-permute-start.12) | collective-permute-done | bytes 262176 | tf_op jit(solution)/shard_map/ppermute | solution.py:627
  217.3 3.4 %collective-permute-start.29 = (f32[2,48,512]{2,1,0:T(8,128)}, f32[2,48,512]{2,1,0:T(8,128)}, u32[]{:S(2)}, u32[]{:S(2)}) collective-permute-start(f32[2,48,512]{2,1,0:T(8,128)} %get-tuple-element.54), channel_id=1, source_target_pairs={{0,32},{4,36},{8,40},{12,44},{16,48},{20,52},{24,56},{28,60},{32,0... | collective-permute-start | bytes 589832 | tf_op jit(solution)/shard_map/ppermute | solution.py:552
  221.5 3.3 %collective-permute-done.29.c2 = f32[2,48,512]{2,1,0:T(8,128)} collective-permute-done((f32[2,48,512]{2,1,0:T(8,128)}, f32[2,48,512]{2,1,0:T(8,128)}, u32[]{:S(2)}, u32[]{:S(2)}) %collective-permute-start.29) | collective-permute-done | bytes 196640 | tf_op jit(solution)/shard_map/ppermute | solution.py:552
  229.9 3.6 %spread.1 = (f32[2,3,64,512]{3,2,1,0:T(8,128)}, f32[2,3,64,512]{3,2,1,0:T(8,128)}, f32[2,3,64,512]{3,2,1,0:T(8,128)}, f32[2,3,64,512]{3,2,1,0:T(8,128)}) custom-call(s32[1]{0:T(128)} %bitcast.6.place, s32[1]{0:T(128)} %bitcast.29.line, f32[6]{0:T(128)} %copy-done.7, f32[6]{0:T(128)} %copy-done.11, f32[6]{0:T(128)} %copy-done.12, f32[6]{0:T(128)} %copy-done.13, ...), custom_call_target="tpu_custom_call" | custom-call | flops 4000000 | bytes 4194304 | tf_op jit(solution)/shard_map/spread/pallas_call | solution.py:501
  233.7 4.5 %collective-permute-start.32 = (f32[2,3,64,512]{3,2,1,0:T(8,128)}, f32[2,3,64,512]{3,2,1,0:T(8,128)}, u32[]{:S(2)}, u32[]{:S(2)}) collective-permute-start(f32[2,3,64,512]{3,2,1,0:T(8,128)} %get-tuple-element.58), channel_id=1, source_target_pairs={{0,8},{4,12},{8,0},{12,4},{16,24},{20,28},{24,16},{28,20},{32,40},... | collective-permute-start | bytes 2359304 | tf_op jit(solution)/shard_map/ppermute | solution.py:545
  238.2 2.8 maximum_select_fusion.fm.am
  241.0 13.9 %collective-permute-done.31.a1 = f32[2,3,64,512]{3,2,1,0:T(8,128)} collective-permute-done((f32[2,3,64,512]{3,2,1,0:T(8,128)}, f32[2,3,64,512]{3,2,1,0:T(8,128)}, u32[]{:S(2)}, u32[]{:S(2)}) %collective-permute-start.31) | collective-permute-done | bytes 786464 | tf_op jit(solution)/shard_map/ppermute | solution.py:545
  256.9 2.8 collective-permute-start.7
  259.7 6.5 %collective-permute-done.33.a3 = f32[2,3,64,512]{3,2,1,0:T(8,128)} collective-permute-done((f32[2,3,64,512]{3,2,1,0:T(8,128)}, f32[2,3,64,512]{3,2,1,0:T(8,128)}, u32[]{:S(2)}, u32[]{:S(2)}) %collective-permute-start.33) | collective-permute-done | bytes 786464 | tf_op jit(solution)/shard_map/ppermute | solution.py:545
  267.7 8.2 %gather_fusion = f32[512]{0:T(512)S(1)} fusion(f32[3,2,256,512]{3,2,1,0:T(8,128)} %bitcast.60, s32[512]{0:T(512)S(1)} %bitcast.66), kind=kCustom, calls=%fused_computation | custom fusion | bytes 12288 | tf_op jit(solution)/shard_map/gather | solution.py:610
  275.9 6.3 %gather_fusion.1 = f32[512]{0:T(512)S(1)} fusion(f32[3,2,256,512]{3,2,1,0:T(8,128)S(1)} %bitcast.61, s32[512]{0:T(512)S(1)} %bitcast.65), kind=kCustom, calls=%fused_computation.1 | custom fusion | bytes 12288 | tf_op jit(solution)/shard_map/gather | solution.py:610
  282.9 4.1 %finish.1 = f32[3,2,256,512]{3,2,1,0:T(8,128)} custom-call(s32[1]{0:T(128)} %bitcast.6.place, f32[3,2,256,512]{3,2,1,0:T(8,128)} %get-tuple-element.34.own, f32[2,3,64,512]{3,2,1,0:T(8,128)} %get-tuple-element.56.a0, f32[2,3,64,512]{3,2,1,0:T(8,128)} %collective-permute-done.31.a1, f32[2,3,64,512]{3,2,1,0:T(8,128)} %collective-permute-done.32.a2, ...), custom_call_target="tpu_custom_call" | custom-call | flops 20000000 | bytes 9437184 | tf_op jit(solution)/shard_map/finish/pallas_call | solution.py:522
  287.0 20.3 %collective-permute-done.5.xr2 = f32[2,2,256,512]{3,2,1,0:T(8,128)} collective-permute-done((f32[2,2,256,512]{3,2,1,0:T(8,128)}, f32[2,2,256,512]{3,2,1,0:T(8,128)}, u32[]{:S(2)}, u32[]{:S(2)}) %collective-permute-start.5) | collective-permute-done | bytes 2097184 | tf_op jit(solution)/shard_map/ppermute | solution.py:585
  307.3 12.3 %products.1 = (f32[3,2,256,512]{3,2,1,0:T(8,128)}, f32[3,2,256,512]{3,2,1,0:T(8,128)}) custom-call(s32[1]{0:T(128)} %bitcast.core, s32[4]{0:T(128)} %add_convert_fusion.second_way, f32[2]{0:T(128)} %gain.7, f32[2]{0:T(128)} %depth.7, f32[2,136,512]{2,1,0:T(8,128)} %copy-done.2, f32[3,2,256,512]{3,2,1,0:T(8,128)} %get-tuple-element.34.own, ...), custom_call_target="tpu_custom_call" | custom-call | flops 48000000 | bytes 25165824 | tf_op jit(solution)/shard_map/products/pallas_call | solution.py:356
  (109 shorter events, 52.3 us)
Async XLA Ops:
  7.7 14.7 %collective-permute-start.1 = (f32[2,136,512]{2,1,0:T(8,128)S(1)}, f32[2,136,512]{2,1,0:T(8,128)S(1)}, u32[]{:S(2)}, u32[]{:S(2)}) collective-permute-start(f32[2,136,512]{2,1,0:T(8,128)S(1)} %add.102), channel_id=1, source_target_pairs={{0,2},{1,3},{2,0},{3,1},{4,6},{5,7},{6,4},{7,5},{8,10},{9,11},{10,... | collective-permute-start | bytes 1671176 | tf_op jit(solution)/shard_map/ppermute | solution.py:540
  23.4 9.4 %collective-permute-start.3 = (f32[2,136,512]{2,1,0:T(8,128)S(1)}, f32[2,136,512]{2,1,0:T(8,128)S(1)}, u32[]{:S(2)}, u32[]{:S(2)}) collective-permute-start(f32[2,136,512]{2,1,0:T(8,128)S(1)} %add.103.mine.depths), channel_id=1, source_target_pairs={{0,1},{1,0},{2,3},{3,2},{4,5},{5,4},{6,7},{7,6},{8,9},{9,8},{10,11... | collective-permute-start | bytes 1671176 | tf_op jit(solution)/shard_map/ppermute | solution.py:540
  23.5 9.2 %collective-permute-start.2 = (f32[6]{0:T(128)S(1)}, f32[6]{0:T(128)S(1)}, u32[]{:S(2)}, u32[]{:S(2)}) collective-permute-start(f32[6]{0:T(128)S(1)} %reshape_squeeze.3), channel_id=1, source_target_pairs={{4,0},{8,4},{12,8},{16,12},{20,16},{24,20},{28,24},{32,28},{36,32}... | collective-permute-start | bytes 80 | tf_op jit(solution)/shard_map/ppermute | solution.py:578
  41.6 66.6 %collective-permute-start.21 = (f32[2,3,64,512]{3,2,1,0:T(8,128)}, f32[2,3,64,512]{3,2,1,0:T(8,128)}, u32[]{:S(2)}, u32[]{:S(2)}) collective-permute-start(f32[2,3,64,512]{3,2,1,0:T(8,128)} %get-tuple-element.45), channel_id=1, source_target_pairs={{0,12},{4,0},{8,4},{12,8},{16,28},{20,16},{24,20},{28,24},{32,44},... | collective-permute-start | bytes 2359304 | tf_op jit(solution)/shard_map/ppermute | solution.py:545
  48.9 55.4 %collective-permute-start.13 = (f32[2,136,512]{2,1,0:T(8,128)}, f32[2,136,512]{2,1,0:T(8,128)S(1)}, u32[]{:S(2)}, u32[]{:S(2)}) collective-permute-start(f32[2,136,512]{2,1,0:T(8,128)} %get-tuple-element.36), channel_id=1, source_target_pairs={{0,1},{1,0},{2,3},{3,2},{4,5},{5,4},{6,7},{7,6},{8,9},{9,8},{10,11... | collective-permute-start | bytes 1671176 | tf_op jit(solution)/shard_map/ppermute | solution.py:540
  52.2 163.8 %collective-permute-start.4 = (f32[2,2,256,512]{3,2,1,0:T(8,128)}, f32[2,2,256,512]{3,2,1,0:T(8,128)}, u32[]{:S(2)}, u32[]{:S(2)}) collective-permute-start(f32[2,2,256,512]{3,2,1,0:T(8,128)} %slice_bitcast_fusion.1), channel_id=1, source_target_pairs={{0,4},{4,8},{8,12},{12,16},{16,20},{20,24},{24,28},{28,32},{32,36}... | collective-permute-start | bytes 6291464 | tf_op jit(solution)/shard_map/ppermute | solution.py:584
  52.3 8.7 %collective-permute-start.18 = (f32[6]{0:T(128)S(1)}, f32[6]{0:T(128)S(1)}, u32[]{:S(2)}, u32[]{:S(2)}) collective-permute-start(f32[6]{0:T(128)S(1)} %copy-done.8), channel_id=1, source_target_pairs={{0,12},{4,0},{8,4},{12,8},{16,28},{20,16},{24,20},{28,24},{32,44},... | collective-permute-start | bytes 80 | tf_op jit(solution)/shard_map/ppermute | solution.py:545
  56.4 43.4 %collective-permute-start.19 = (f32[6]{0:T(128)S(1)}, f32[6]{0:T(128)S(1)}, u32[]{:S(2)}, u32[]{:S(2)}) collective-permute-start(f32[6]{0:T(128)S(1)} %copy-done.8), channel_id=1, source_target_pairs={{0,8},{4,12},{8,0},{12,4},{16,24},{20,28},{24,16},{28,20},{32,40},... | collective-permute-start | bytes 80 | tf_op jit(solution)/shard_map/ppermute | solution.py:545
  61.0 41.2 %collective-permute-start.20 = (f32[6]{0:T(128)S(1)}, f32[6]{0:T(128)S(1)}, u32[]{:S(2)}, u32[]{:S(2)}) collective-permute-start(f32[6]{0:T(128)S(1)} %copy-done.8), channel_id=1, source_target_pairs={{0,4},{4,8},{8,12},{12,0},{16,20},{20,24},{24,28},{28,16},{32,36},... | collective-permute-start | bytes 80 | tf_op jit(solution)/shard_map/ppermute | solution.py:545
  99.9 22.3 %collective-permute-start.22 = (f32[2,3,64,512]{3,2,1,0:T(8,128)}, f32[2,3,64,512]{3,2,1,0:T(8,128)}, u32[]{:S(2)}, u32[]{:S(2)}) collective-permute-start(f32[2,3,64,512]{3,2,1,0:T(8,128)} %get-tuple-element.46), channel_id=1, source_target_pairs={{0,8},{4,12},{8,0},{12,4},{16,24},{20,28},{24,16},{28,20},{32,40},... | collective-permute-start | bytes 2359304 | tf_op jit(solution)/shard_map/ppermute | solution.py:545
  102.8 34.8 %collective-permute-start.23 = (f32[2,3,64,512]{3,2,1,0:T(8,128)S(1)}, f32[2,3,64,512]{3,2,1,0:T(8,128)}, u32[]{:S(2)}, u32[]{:S(2)}) collective-permute-start(f32[2,3,64,512]{3,2,1,0:T(8,128)S(1)} %copy-done.17), channel_id=1, source_target_pairs={{0,4},{4,8},{8,12},{12,0},{16,20},{20,24},{24,28},{28,16},{32,36},... | collective-permute-start | bytes 2359304 | tf_op jit(solution)/shard_map/ppermute | solution.py:545
  104.3 113.1 %collective-permute-start.8 = (f32[2,2,256,512]{3,2,1,0:T(8,128)}, f32[2,2,256,512]{3,2,1,0:T(8,128)}, u32[]{:S(2)}, u32[]{:S(2)}) collective-permute-start(f32[2,2,256,512]{3,2,1,0:T(8,128)} %slice_bitcast_fusion), channel_id=1, source_target_pairs={{0,60},{4,0},{8,4},{12,8},{16,12},{20,16},{24,20},{28,24},{32,28},... | collective-permute-start | bytes 6291464 | tf_op jit(solution)/shard_map/ppermute | solution.py:584
  108.2 35.9 %collective-permute-start.14 = (f32[2,136,512]{2,1,0:T(8,128)}, f32[2,136,512]{2,1,0:T(8,128)}, u32[]{:S(2)}, u32[]{:S(2)}) collective-permute-start(f32[2,136,512]{2,1,0:T(8,128)} %add.105), channel_id=1, source_target_pairs={{0,2},{1,3},{2,0},{3,1},{4,6},{5,7},{6,4},{7,5},{8,10},{9,11},{10,... | collective-permute-start | bytes 1671176 | tf_op jit(solution)/shard_map/ppermute | solution.py:540
  140.3 20.4 %collective-permute-start.24 = (f32[2,56,512]{2,1,0:T(8,128)}, f32[2,56,512]{2,1,0:T(8,128)}, u32[]{:S(2)}, u32[]{:S(2)}) collective-permute-start(f32[2,56,512]{2,1,0:T(8,128)} %get-tuple-element.49), channel_id=1, source_target_pairs={{0,48},{4,52},{8,56},{12,60},{16,0},{20,4},{24,8},{28,12},{32,16},... | collective-permute-start | bytes 688136 | tf_op jit(solution)/shard_map/ppermute | solution.py:552
  141.6 19.1 %collective-permute-start.25 = (f32[2,56,512]{2,1,0:T(8,128)}, f32[2,56,512]{2,1,0:T(8,128)}, u32[]{:S(2)}, u32[]{:S(2)}) collective-permute-start(f32[2,56,512]{2,1,0:T(8,128)} %get-tuple-element.50), channel_id=1, source_target_pairs={{0,32},{4,36},{8,40},{12,44},{16,48},{20,52},{24,56},{28,60},{32,0... | collective-permute-start | bytes 688136 | tf_op jit(solution)/shard_map/ppermute | solution.py:552
  144.1 20.5 %collective-permute-start.26 = (f32[2,56,512]{2,1,0:T(8,128)}, f32[2,56,512]{2,1,0:T(8,128)}, u32[]{:S(2)}, u32[]{:S(2)}) collective-permute-start(f32[2,56,512]{2,1,0:T(8,128)} %get-tuple-element.51), channel_id=1, source_target_pairs={{0,16},{4,20},{8,24},{12,28},{16,32},{20,36},{24,40},{28,44},{32,4... | collective-permute-start | bytes 688136 | tf_op jit(solution)/shard_map/ppermute | solution.py:552
  160.7 72.9 %collective-permute-start.10 = (f32[1,2,256,512]{3,2,1,0:T(8,128)}, f32[1,2,256,512]{3,2,1,0:T(8,128)}, u32[]{:S(2)}, u32[]{:S(2)}) collective-permute-start(f32[1,2,256,512]{3,2,1,0:T(8,128)} %slice_bitcast_fusion.2), channel_id=1, source_target_pairs={{0,12},{4,0},{8,4},{12,8},{16,28},{20,16},{24,20},{28,24},{32,44},... | collective-permute-start | bytes 3145736 | tf_op jit(solution)/shard_map/ppermute | solution.py:545
  160.7 27.0 %collective-permute-start.15 = (f32[2,64,512]{2,1,0:T(8,128)}, f32[2,64,512]{2,1,0:T(8,128)}, u32[]{:S(2)}, u32[]{:S(2)}) collective-permute-start(f32[2,64,512]{2,1,0:T(8,128)} %dynamic-slice_add_fusion), channel_id=1, source_target_pairs={{4,0},{8,4},{12,8},{16,12},{20,16},{24,20},{28,24},{32,28},{36,32}... | collective-permute-start | bytes 786440 | tf_op jit(solution)/shard_map/ppermute | solution.py:630
  166.6 22.7 %collective-permute-start.27 = (f32[2,48,512]{2,1,0:T(8,128)}, f32[2,48,512]{2,1,0:T(8,128)}, u32[]{:S(2)}, u32[]{:S(2)}) collective-permute-start(f32[2,48,512]{2,1,0:T(8,128)} %half_total.1), channel_id=1, source_target_pairs={{0,64},{4,68},{8,72},{12,76},{16,80},{20,84},{24,88},{28,92},{32,9... | collective-permute-start | bytes 589832 | tf_op jit(solution)/shard_map/ppermute | solution.py:559
  187.6 46.0 %collective-permute-start.6 = (f32[1,2,256,512]{3,2,1,0:T(8,128)}, f32[1,2,256,512]{3,2,1,0:T(8,128)}, u32[]{:S(2)}, u32[]{:S(2)}) collective-permute-start(f32[1,2,256,512]{3,2,1,0:T(8,128)} %slice_bitcast_fusion.3), channel_id=1, source_target_pairs={{0,4},{4,8},{8,12},{12,0},{16,20},{20,24},{24,28},{28,16},{32,36},... | collective-permute-start | bytes 3145736 | tf_op jit(solution)/shard_map/ppermute | solution.py:545
  189.3 22.2 %collective-permute-start.12 = (f32[2,64,512]{2,1,0:T(8,128)}, f32[2,64,512]{2,1,0:T(8,128)}, u32[]{:S(2)}, u32[]{:S(2)}) collective-permute-start(f32[2,64,512]{2,1,0:T(8,128)} %constant_dynamic-slice_fusion), channel_id=1, source_target_pairs={{0,4},{4,8},{8,12},{12,16},{16,20},{20,24},{24,28},{28,32},{32,36}... | collective-permute-start | bytes 786440 | tf_op jit(solution)/shard_map/ppermute | solution.py:627
  211.6 9.2 %collective-permute-start.28 = (f32[2,48,512]{2,1,0:T(8,128)}, f32[2,48,512]{2,1,0:T(8,128)}, u32[]{:S(2)}, u32[]{:S(2)}) collective-permute-start(f32[2,48,512]{2,1,0:T(8,128)} %get-tuple-element.53), channel_id=1, source_target_pairs={{0,48},{4,52},{8,56},{12,60},{16,0},{20,4},{24,8},{28,12},{32,16},... | collective-permute-start | bytes 589832 | tf_op jit(solution)/shard_map/ppermute | solution.py:552
  216.1 22.1 %collective-permute-start.16 = (f32[4,64,512]{2,1,0:T(8,128)}, f32[4,64,512]{2,1,0:T(8,128)}, u32[]{:S(2)}, u32[]{:S(2)}) collective-permute-start(f32[4,64,512]{2,1,0:T(8,128)} %constant_dynamic-update-slice_fusion), channel_id=1, source_target_pairs={{0,2},{1,3},{2,0},{3,1},{4,6},{5,7},{6,4},{7,5},{8,10},{9,11},{10,... | collective-permute-start | bytes 1572872 | tf_op jit(solution)/shard_map/ppermute | solution.py:540
  217.3 7.5 %collective-permute-start.29 = (f32[2,48,512]{2,1,0:T(8,128)}, f32[2,48,512]{2,1,0:T(8,128)}, u32[]{:S(2)}, u32[]{:S(2)}) collective-permute-start(f32[2,48,512]{2,1,0:T(8,128)} %get-tuple-element.54), channel_id=1, source_target_pairs={{0,32},{4,36},{8,40},{12,44},{16,48},{20,52},{24,56},{28,60},{32,0... | collective-permute-start | bytes 589832 | tf_op jit(solution)/shard_map/ppermute | solution.py:552
  224.8 82.5 %collective-permute-start.5 = (f32[2,2,256,512]{3,2,1,0:T(8,128)}, f32[2,2,256,512]{3,2,1,0:T(8,128)}, u32[]{:S(2)}, u32[]{:S(2)}) collective-permute-start(f32[2,2,256,512]{3,2,1,0:T(8,128)} %collective-permute-done.4.xr), channel_id=1, source_target_pairs={{0,64},{1,65},{2,66},{3,67}} | collective-permute-start | bytes 6291464 | tf_op jit(solution)/shard_map/ppermute | solution.py:585
  227.9 79.4 %collective-permute-start.9 = (f32[2,2,256,512]{3,2,1,0:T(8,128)}, f32[2,2,256,512]{3,2,1,0:T(8,128)}, u32[]{:S(2)}, u32[]{:S(2)}) collective-permute-start(f32[2,2,256,512]{3,2,1,0:T(8,128)} %collective-permute-done.8.lr), channel_id=1, source_target_pairs={{124,60},{125,61},{126,62},{127,63}} | collective-permute-start | bytes 6291464 | tf_op jit(solution)/shard_map/ppermute | solution.py:585
  233.6 21.3 %collective-permute-start.31 = (f32[2,3,64,512]{3,2,1,0:T(8,128)}, f32[2,3,64,512]{3,2,1,0:T(8,128)}, u32[]{:S(2)}, u32[]{:S(2)}) collective-permute-start(f32[2,3,64,512]{3,2,1,0:T(8,128)} %get-tuple-element.57), channel_id=1, source_target_pairs={{0,12},{4,0},{8,4},{12,8},{16,28},{20,16},{24,20},{28,24},{32,44},... | collective-permute-start | bytes 2359304 | tf_op jit(solution)/shard_map/ppermute | solution.py:545
  233.7 23.2 %collective-permute-start.32 = (f32[2,3,64,512]{3,2,1,0:T(8,128)}, f32[2,3,64,512]{3,2,1,0:T(8,128)}, u32[]{:S(2)}, u32[]{:S(2)}) collective-permute-start(f32[2,3,64,512]{3,2,1,0:T(8,128)} %get-tuple-element.58), channel_id=1, source_target_pairs={{0,8},{4,12},{8,0},{12,4},{16,24},{20,28},{24,16},{28,20},{32,40},... | collective-permute-start | bytes 2359304 | tf_op jit(solution)/shard_map/ppermute | solution.py:545
  238.2 28.1 %collective-permute-start.33 = (f32[2,3,64,512]{3,2,1,0:T(8,128)}, f32[2,3,64,512]{3,2,1,0:T(8,128)}, u32[]{:S(2)}, u32[]{:S(2)}) collective-permute-start(f32[2,3,64,512]{3,2,1,0:T(8,128)} %get-tuple-element.59), channel_id=1, source_target_pairs={{0,4},{4,8},{8,12},{12,0},{16,20},{20,24},{24,28},{28,16},{32,36},... | collective-permute-start | bytes 2359304 | tf_op jit(solution)/shard_map/ppermute | solution.py:545
  254.8 32.1 %collective-permute-start.11 = (f32[1,2,256,512]{3,2,1,0:T(8,128)}, f32[1,2,256,512]{3,2,1,0:T(8,128)}, u32[]{:S(2)}, u32[]{:S(2)}) collective-permute-start(f32[1,2,256,512]{3,2,1,0:T(8,128)} %collective-permute-done.10.lv), channel_id=1, source_target_pairs={{28,12},{44,28},{60,44},{76,60},{92,76},{108,92},{124,108},{29,13}... | collective-permute-start | bytes 3145736 | tf_op jit(solution)/shard_map/ppermute | solution.py:588
  256.9 30.1 %collective-permute-start.7 = (f32[1,2,256,512]{3,2,1,0:T(8,128)}, f32[1,2,256,512]{3,2,1,0:T(8,128)}, u32[]{:S(2)}, u32[]{:S(2)}) collective-permute-start(f32[1,2,256,512]{3,2,1,0:T(8,128)} %collective-permute-done.6.xv), channel_id=1, source_target_pairs={{0,16},{16,32},{32,48},{48,64},{64,80},{80,96},{96,112},{1,17},{17... | collective-permute-start | bytes 3145736 | tf_op jit(solution)/shard_map/ppermute | solution.py:588
  266.3 20.7 %collective-permute-start.17 = (f32[4,128,512]{2,1,0:T(8,128)}, f32[4,128,512]{2,1,0:T(8,128)}, u32[]{:S(2)}, u32[]{:S(2)}) collective-permute-start(f32[4,128,512]{2,1,0:T(8,128)} %maximum_select_fusion.fm.am), channel_id=1, source_target_pairs={{0,1},{1,0},{2,3},{3,2},{4,5},{5,4},{6,7},{7,6},{8,9},{9,8},{10,11... | collective-permute-start | bytes 3145736 | tf_op jit(solution)/shard_map/ppermute | solution.py:540
  (20 other events, 603.3 us)
